TPU v7x, 32 devices: a whole 2x2x4 slice. The times are simulated.
32 devices in a mesh: nest: 2 (over core), row: 4 (over y, x), col: 4 (over z).
Axes of the slice: x: 2, y: 2, z: 4, core: 2. Of those that a mesh axis runs over, the one named last changes fastest.
Arguments:
- strips: float32 [2, 3, 4, 16, 24, 1536], P('nest', None, None, ('row', 'col')), may hold values from -1.5 to 2, as said below
- anchor: int32 [2, 2], replicated, may hold values from 1 to 127
- wet_mask: int32 [2, 512, 512], P('nest', 'row', 'col'), may hold values 0 or 1
- bathy_index: int32 [2, 512, 512], P('nest', 'row', 'col'), may hold values from 0 to 15
- bed_levels: float32 [16], replicated, may hold values from 0 to 1.5
- coarse: float32 [3, 1024, 512], P(None, ('nest', 'row'), 'col'), may hold values from -6 to 6
Outputs:
- fine_fields: float32 [2, 3, 1536, 1536], P('nest', None, 'row', 'col')
- coarse_next: float32 [3, 1024, 512], P(None, ('nest', 'row'), 'col')
Inputs may be any that keep to these rules, and one draw needn't show every extreme that they name: `strips`: plane 0 of the second dimension is the water depth, within 0.5 to 2; planes 1 and 2 are momenta within -1.5 to 1.5. anchor[n] holds the row and then the column offset of nest n's first coarse cell within its block of coarse rows.
All inputs are finite; a program needn't handle non-finite values. No bound on the sum of `wet_mask` on one device may be relied on, other than what follows from the above.
Results may differ from a plain program's by a relative error of at most 0.0003.
Values sent between devices are 32-bit elements; how exact they have to be, the bound alone decides.
No kernel may reach another device: no remote copies, remote signals or barrier semaphores. Data moves between devices by JAX's collectives and lax.ppermute only.
A program may use at most 128 MiB of HBM per device.

v0:
```python
import jax
import jax.numpy as jnp
from jax import lax
from jax.sharding import PartitionSpec as P

gravity = 1.0
courant = 0.2


def padded_2(cells, sides, width):
    for axis, dim in sides:
        count = lax.axis_size(axis)
        ends = count - 1
        head = lax.slice_in_dim(cells, 0, width, axis=dim)
        tail = lax.slice_in_dim(cells, cells.shape[dim] - width, cells.shape[dim], axis=dim)
        cells = jnp.concatenate(
            [
                lax.ppermute(tail, axis, [(i, (i + 1) % count) for i in range(ends)]),
                cells,
                lax.ppermute(head, axis, [((i + 1) % count, i) for i in range(ends)]),
            ],
            axis=dim,
        )
    return cells


def passed_along(block, axis, distance):
    devices = range(lax.axis_size(axis))
    route = [(i - distance, i) for i in devices if i - distance in devices]
    return lax.ppermute(block, axis, route)


def advance(padded, bed_pad, wet_pad):
    depth_now = padded[0]
    flow_u = padded[1]
    flow_v = padded[2]
    depth_safe = jnp.where(wet_pad > 0.5, depth_now, 1.0)
    speed_u = flow_u / depth_safe
    speed_v = flow_v / depth_safe
    celerity = jnp.sqrt(gravity * depth_safe)
    pressure = 0.5 * gravity * depth_safe * depth_safe
    fluxes_x = (flow_u, flow_u * speed_u + pressure, flow_v * speed_u)
    fluxes_y = (flow_v, flow_u * speed_v, flow_v * speed_v + pressure)
    reach_x = jnp.abs(speed_u) + celerity
    reach_y = jnp.abs(speed_v) + celerity
    open_x = wet_pad[1:-1, :-1] * wet_pad[1:-1, 1:]
    open_y = wet_pad[:-1, 1:-1] * wet_pad[1:, 1:-1]
    bound_x = jnp.maximum(reach_x[1:-1, :-1], reach_x[1:-1, 1:])
    bound_y = jnp.maximum(reach_y[:-1, 1:-1], reach_y[1:, 1:-1])
    slope_x = (bed_pad[1:-1, 1:] - bed_pad[1:-1, :-1]) * open_x
    slope_y = (bed_pad[1:, 1:-1] - bed_pad[:-1, 1:-1]) * open_y
    centre = depth_now[1:-1, 1:-1]
    sources = (
        None,
        -0.5 * gravity * centre * (slope_x[:, 1:] + slope_x[:, :-1]),
        -0.5 * gravity * centre * (slope_y[1:] + slope_y[:-1]),
    )
    results = []
    for plane in range(3):
        state = padded[plane]
        flux_col = fluxes_x[plane]
        flux_row = fluxes_y[plane]
        face_x = (
            0.5 * (flux_col[1:-1, :-1] + flux_col[1:-1, 1:])
            - 0.5 * bound_x * (state[1:-1, 1:] - state[1:-1, :-1])
        ) * open_x
        face_y = (
            0.5 * (flux_row[:-1, 1:-1] + flux_row[1:, 1:-1])
            - 0.5 * bound_y * (state[1:, 1:-1] - state[:-1, 1:-1])
        ) * open_y
        value = (
            state[1:-1, 1:-1]
            - courant * (face_x[:, 1:] - face_x[:, :-1])
            - courant * (face_y[1:] - face_y[:-1])
        )
        if plane > 0:
            value = value + courant * sources[plane]
        results.append(value)
    return jnp.stack(results)


def expand(cells):
    return jnp.repeat(jnp.repeat(cells, 3, axis=-2), 3, axis=-1)


def lookup(classes, levels):
    ladder = jnp.arange(levels.shape[0], dtype=jnp.int32)
    matches = classes[None] == ladder[:, None, None]
    return jnp.sum(jnp.where(matches, levels[:, None, None], 0.0), axis=0)


def restrict(updated):
    planes, row_count, col_count = updated.shape
    return updated.reshape(planes, row_count // 3, 3, col_count // 3, 3).sum(axis=(2, 4)) / 9.0


def local(strips, anchor, wet_mask, bathy_index, bed_levels, coarse):
    tile_blocks = strips.shape[2]
    band_rows = strips.shape[4]
    full_cols = strips.shape[5]
    columns = lax.axis_size("col")
    tile_cols = full_cols // columns
    layered = (
        strips[0, :, :, 0]
        .reshape(3, tile_blocks, band_rows, columns, tile_cols)
        .transpose(0, 1, 3, 2, 4)
    )
    flattened = layered.reshape(3, tile_blocks * columns, band_rows, tile_cols)
    arrived = lax.all_to_all(flattened, ("row", "col"), split_axis=1, concat_axis=1, tiled=True)
    fields = arrived.reshape(3, tile_blocks * columns * band_rows, tile_cols)
    classes = bathy_index[0]
    wet_cells = wet_mask[0]
    bed_fine = expand(lookup(classes, bed_levels))
    wetness = expand(wet_cells.astype(jnp.float32))
    stacked = jnp.concatenate([fields, bed_fine[None], wetness[None]], axis=0)
    padded_all = padded_2(stacked, (("row", 1), ("col", 2)), 1)
    padded = padded_all[:3]
    bed_pad = padded_all[3]
    wet_pad = padded_all[4]
    updated = advance(padded, bed_pad, wet_pad)
    restricted = restrict(updated)
    coarse_rows = restricted.shape[1]
    coarse_cols = restricted.shape[2]
    contribution = jnp.concatenate(
        [restricted, jnp.ones((1, coarse_rows, coarse_cols), jnp.float32)], axis=0
    )
    nest_index = lax.axis_index("nest")
    corner = lax.dynamic_index_in_dim(anchor, nest_index, 0, keepdims=False)
    canvas = lax.dynamic_update_slice(
        jnp.zeros((4, 2 * coarse_rows, 2 * coarse_cols), jnp.float32),
        contribution,
        (jnp.int32(0), corner[0], corner[1]),
    )
    spilled = passed_along(canvas[:, :, coarse_cols:], "col", 1)
    merged = canvas[:, :, :coarse_cols] + spilled
    lowered = passed_along(merged[:, coarse_rows:], ("nest", "row"), 1)
    received_sum = merged[:, :coarse_rows] + lowered
    coarse_next = (coarse + received_sum[:3]) / (1.0 + received_sum[3])
    return (updated[None], coarse_next)


def solution(mesh):
    return jax.shard_map(
        local,
        mesh=mesh,
        in_specs=(
            P("nest", None, None, ("row", "col"), None, None),
            P(),
            P("nest", "row", "col"),
            P("nest", "row", "col"),
            P(),
            P(None, ("nest", "row"), "col"),
        ),
        out_specs=(P("nest", None, "row", "col"), P(None, ("nest", "row"), "col")),
        check_vma=False,
    )
```

profile of v0, /device:TPU:12, one launch (start us, length us, event | category | flops | bytes accessed | tf_op | source)
XLA Modules:
  0.0 250.1 jit_solution(6298156898916044480)
XLA Ops:
  0.6 1.9 reshape_squeeze.3
  3.9 7.3 %all-to-all-start = ((f32[3,16,24,384]{3,2,0,1:T(8,128)}), f32[3,16,24,384]{3,2,0,1:T(8,128)}, u32[]{:S(2)}, u32[]{:S(2)}) async-start(f32[3,16,24,384]{3,2,0,1:T(8,128)} %bitcast.1), calls=%async_computation | async-start | bytes 3538944 | tf_op jit(solution)/shard_map/all_to_all | solution.py:109
  13.3 36.6 %all-to-all-done = f32[3,16,24,384]{3,2,0,1:T(8,128)} async-done(((f32[3,16,24,384]{3,2,0,1:T(8,128)}), f32[3,16,24,384]{3,2,0,1:T(8,128)}, u32[]{:S(2)}, u32[]{:S(2)}) %all-to-all-start) | async-done | bytes 1769504 | tf_op jit(solution)/shard_map/all_to_all | solution.py:109
  50.0 1.6 copy.38
  51.6 3.1 %collective-permute-start.1 = (f32[5,1,384]{2,1,0:T(1,128)S(1)}, f32[5,1,384]{2,1,0:T(1,128)S(1)}, u32[]{:S(2)}, u32[]{:S(2)}) collective-permute-start(f32[5,1,384]{2,1,0:T(1,128)S(1)} %get-tuple-element.23), channel_id=1, source_target_pairs={{4,0},{8,4},{12,8},{5,1},{9,5},{13,9},{6,2},{10,6},{14,10},{7,3},{... | collective-permute-start | bytes 23048 | tf_op jit(solution)/shard_map/ppermute | solution.py:20
  54.7 2.8 %collective-permute-start = (f32[5,1,384]{2,1,0:T(1,128)S(1)}, f32[5,1,384]{2,1,0:T(1,128)S(1)}, u32[]{:S(2)}, u32[]{:S(2)}) collective-permute-start(f32[5,1,384]{2,1,0:T(1,128)S(1)} %get-tuple-element.22), channel_id=1, source_target_pairs={{0,4},{4,8},{8,12},{1,5},{5,9},{9,13},{2,6},{6,10},{10,14},{3,7},{... | collective-permute-start | bytes 23048 | tf_op jit(solution)/shard_map/ppermute | solution.py:18
  57.5 3.6 %collective-permute-done = f32[5,1,384]{2,1,0:T(1,128)S(1)} collective-permute-done((f32[5,1,384]{2,1,0:T(1,128)S(1)}, f32[5,1,384]{2,1,0:T(1,128)S(1)}, u32[]{:S(2)}, u32[]{:S(2)}) %collective-permute-start) | collective-permute-done | bytes 7712 | tf_op jit(solution)/shard_map/ppermute | solution.py:18
  61.1 1.6 pad_maximum_fusion.5
  62.7 1.6 copy.44
  64.3 4.7 %collective-permute-start.3 = (f32[5,386,1]{1,2,0:T(1,128)S(1)}, f32[5,386,1]{1,2,0:T(1,128)S(1)}, u32[]{:S(2)}, u32[]{:S(2)}) collective-permute-start(f32[5,386,1]{1,2,0:T(1,128)S(1)} %copy.44), channel_id=1, source_target_pairs={{1,0},{2,1},{3,2},{5,4},{6,5},{7,6},{9,8},{10,9},{11,10},{13,12},{... | collective-permute-start | bytes 23168 | tf_op jit(solution)/shard_map/ppermute | solution.py:20
  69.0 1.6 copy.43
  70.7 2.1 collective-permute-start.2
  77.2 1.3 copy.46
  78.6 1.4 copy.45
  79.9 5.5 %pad_maximum_fusion = f32[5,386,386]{2,1,0:T(8,128)S(1)} fusion(f32[5,386,1]{2,1,0:T(8,128)} %copy.46, f32[5,1,384]{2,1,0:T(1,128)S(1)} %collective-permute-done.1, f32[1,384,384]{2,1,0:T(8,128)S(1)} %copy.42, f32[1,384,384]{2,1,0:T(8,128)S(1)} %copy.41, f32[3,384,384]{2,1,0:T(8,128)S(1)} %bitcast.64, f32[5,1,384]{2,1,0:T(1,128)S(1)} %collective-permute-done, ...), kind=kLoop, calls=%fused_computation | loop fusion | flops 4469880 | bytes 5959840 | tf_op jit(solution)/shard_map/concatenate | solution.py:16
  86.7 2.2 fusion.22
  88.9 1.9 fusion.10
  90.8 2.8 %fusion.18 = (f32[385,384]{1,0:T(8,128)}, f32[385,384]{1,0:T(8,128)S(1)}, f32[385,384]{1,0:T(8,128)S(1)}) fusion(f32[385,384]{1,0:T(8,128)S(1)} %get-tuple-element.7, f32[386,386]{1,0:T(8,128)S(1)} %get-tuple-element.15, f32[386,386]{1,0:T(8,128)S(1)} %get-tuple-element.10, f32[386,386]{1,0:T(8,128)S(1)} %get-tuple-element.14, ...), kind=kLoop, calls=%fused_computation.49 | loop fusion | flops 2365440 | bytes 9461760 | tf_op jit(solution)/shard_map/mul | solution.py:67
  93.6 2.7 %fusion.7 = (f32[384,385]{1,0:T(8,128)}, f32[384,385]{1,0:T(8,128)S(1)}, f32[384,385]{1,0:T(8,128)}) fusion(f32[384,385]{1,0:T(8,128)S(1)} %get-tuple-element.5, f32[386,386]{1,0:T(8,128)S(1)} %get-tuple-element.8, f32[386,386]{1,0:T(8,128)S(1)} %get-tuple-element.15, f32[386,386]{1,0:T(8,128)S(1)} %get-tuple-element.13, ...), kind=kLoop, calls=%fused_computation.32 | loop fusion | flops 2365440 | bytes 9461760 | tf_op jit(solution)/shard_map/mul | solution.py:63
  96.9 25.2 %stack.26 = f32[1,128,3,128,3]{4,3,2,1,0:T(8,128)} reshape(f32[384,384]{1,0:T(8,128)S(1)} %fusion.26) | data formatting | bytes 1179648 | tf_op jit(solution)/shard_map/stack | solution.py:79
  122.1 15.5 %copy.49 = f32[1,128,3,128,3]{3,1,4,2,0:T(8,128)} copy(f32[1,128,3,128,3]{4,3,2,1,0:T(8,128)} %stack.26) | data formatting | bytes 1179648 | tf_op jit(solution)/shard_map/stack | solution.py:79
  137.6 3.8 %fusion.39 = (f32[384,384]{1,0:T(8,128)S(1)}, f32[384,384]{1,0:T(8,128)S(1)}) fusion(f32[385,384]{1,0:T(8,128)} %get-tuple-element.6, f32[384,385]{1,0:T(8,128)} %get-tuple-element.4, f32[386,386]{1,0:T(8,128)S(1)} %get-tuple-element.19, f32[384,385]{1,0:T(8,128)} %get-tuple-element.30, f32[385,384]{1,0:T(8,128)} %get-tuple-element.26, ...), kind=kLoop, calls=%fused_computation.81 | loop fusion | flops 2506752 | bytes 8257536 | tf_op jit(solution)/shard_map/sub | solution.py:72
  141.4 25.2 %stack.25 = f32[1,128,3,128,3]{4,3,2,1,0:T(8,128)} reshape(f32[384,384]{1,0:T(8,128)S(1)} %get-tuple-element.29) | data formatting | bytes 1179648 | tf_op jit(solution)/shard_map/stack | solution.py:79
  166.6 14.8 %copy.48 = f32[1,128,3,128,3]{3,1,4,2,0:T(8,128)S(1)} copy(f32[1,128,3,128,3]{4,3,2,1,0:T(8,128)} %stack.25) | data formatting | bytes 1179648 | tf_op jit(solution)/shard_map/stack | solution.py:79
  181.4 25.2 %stack.24 = f32[1,128,3,128,3]{4,3,2,1,0:T(8,128)} reshape(f32[384,384]{1,0:T(8,128)S(1)} %get-tuple-element.28) | data formatting | bytes 1179648 | tf_op jit(solution)/shard_map/stack | solution.py:79
  206.6 15.5 %copy.47 = f32[1,128,3,128,3]{3,1,4,2,0:T(8,128)} copy(f32[1,128,3,128,3]{4,3,2,1,0:T(8,128)} %stack.24) | data formatting | bytes 1179648 | tf_op jit(solution)/shard_map/stack | solution.py:79
  223.5 3.3 %dynamic_update_slice.3 = f32[4,256,256]{2,1,0:T(8,128)S(1)} dynamic-update-slice(f32[4,256,256]{2,1,0:T(8,128)S(1)} %broadcast_in_dim.46, f32[4,128,128]{2,1,0:T(8,128)S(1)} %concatenate.16, s32[]{:T(128)} %constant.5.clone.1, s32[]{:T(128)S(6)} %select_n.21, s32[]{:T(128)S(6)} %select_n.22) | dynamic-update-slice | bytes 524292 | tf_op jit(solution)/shard_map/dynamic_update_slice | solution.py:129
  226.8 2.6 %collective-permute-start.4 = (f32[4,256,128]{2,1,0:T(8,128)S(1)}, f32[4,256,128]{2,1,0:T(8,128)S(1)}, u32[]{:S(2)}, u32[]{:S(2)}) collective-permute-start(f32[4,256,128]{2,1,0:T(8,128)S(1)} %slice.343), channel_id=1, source_target_pairs={{0,1},{1,2},{2,3},{4,5},{5,6},{6,7},{8,9},{9,10},{10,11},{12,13},{... | collective-permute-start | bytes 1572872 | tf_op jit(solution)/shard_map/ppermute | solution.py:30
  229.4 10.6 %collective-permute-done.4 = f32[4,256,128]{2,1,0:T(8,128)S(1)} collective-permute-done((f32[4,256,128]{2,1,0:T(8,128)S(1)}, f32[4,256,128]{2,1,0:T(8,128)S(1)}, u32[]{:S(2)}, u32[]{:S(2)}) %collective-permute-start.4) | collective-permute-done | bytes 524320 | tf_op jit(solution)/shard_map/ppermute | solution.py:30
  240.2 2.5 collective-permute-start.5
  242.7 1.3 maximum_bitcast_fusion
  244.0 5.4 %collective-permute-done.5 = f32[4,128,128]{2,1,0:T(8,128)S(1)} collective-permute-done((f32[4,128,128]{2,1,0:T(8,128)S(1)}, f32[4,128,128]{2,1,0:T(8,128)S(1)}, u32[]{:S(2)}, u32[]{:S(2)}) %collective-permute-start.5) | collective-permute-done | bytes 262176 | tf_op jit(solution)/shard_map/ppermute | solution.py:30
  (49 shorter events, 8.1 us)
Async XLA Ops:
  0.6 56.8 %copy-start = (s32[2,2]{1,0:T(2,128)S(1)}, s32[2,2]{1,0:T(2,128)}, u32[]{:S(2)}) copy-start(s32[2,2]{1,0:T(2,128)} %param.7) | copy-start | bytes 52
  2.5 8.6 %copy-start.4 = (s32[1,128,128]{2,1,0:T(8,128)S(1)}, s32[1,128,128]{2,1,0:T(8,128)}, u32[]{:S(2)}) copy-start(s32[1,128,128]{2,1,0:T(8,128)} %param.8) | copy-start | bytes 196612
  3.9 8.3 %copy-start.5 = (s32[1,128,128]{2,1,0:T(8,128)S(1)}, s32[1,128,128]{2,1,0:T(8,128)}, u32[]{:S(2)}) copy-start(s32[1,128,128]{2,1,0:T(8,128)} %param.9) | copy-start | bytes 196612
  3.9 8.3 %copy-start.6 = (f32[16]{0:T(128)S(1)}, f32[16]{0:T(128)}, u32[]{:S(2)}) copy-start(f32[16]{0:T(128)} %param.10) | copy-start | bytes 196
  3.9 46.1 %all-to-all-start = ((f32[3,16,24,384]{3,2,0,1:T(8,128)}), f32[3,16,24,384]{3,2,0,1:T(8,128)}, u32[]{:S(2)}, u32[]{:S(2)}) async-start(f32[3,16,24,384]{3,2,0,1:T(8,128)} %bitcast.1), calls=%async_computation | async-start | bytes 3538944 | tf_op jit(solution)/shard_map/all_to_all | solution.py:109
  51.6 5.9 %collective-permute-start.1 = (f32[5,1,384]{2,1,0:T(1,128)S(1)}, f32[5,1,384]{2,1,0:T(1,128)S(1)}, u32[]{:S(2)}, u32[]{:S(2)}) collective-permute-start(f32[5,1,384]{2,1,0:T(1,128)S(1)} %get-tuple-element.23), channel_id=1, source_target_pairs={{4,0},{8,4},{12,8},{5,1},{9,5},{13,9},{6,2},{10,6},{14,10},{7,3},{... | collective-permute-start | bytes 23048 | tf_op jit(solution)/shard_map/ppermute | solution.py:20
  54.7 6.4 %collective-permute-start = (f32[5,1,384]{2,1,0:T(1,128)S(1)}, f32[5,1,384]{2,1,0:T(1,128)S(1)}, u32[]{:S(2)}, u32[]{:S(2)}) collective-permute-start(f32[5,1,384]{2,1,0:T(1,128)S(1)} %get-tuple-element.22), channel_id=1, source_target_pairs={{0,4},{4,8},{8,12},{1,5},{5,9},{9,13},{2,6},{6,10},{10,14},{3,7},{... | collective-permute-start | bytes 23048 | tf_op jit(solution)/shard_map/ppermute | solution.py:18
  64.3 12.9 %collective-permute-start.3 = (f32[5,386,1]{1,2,0:T(1,128)S(1)}, f32[5,386,1]{1,2,0:T(1,128)S(1)}, u32[]{:S(2)}, u32[]{:S(2)}) collective-permute-start(f32[5,386,1]{1,2,0:T(1,128)S(1)} %copy.44), channel_id=1, source_target_pairs={{1,0},{2,1},{3,2},{5,4},{6,5},{7,6},{9,8},{10,9},{11,10},{13,12},{... | collective-permute-start | bytes 23168 | tf_op jit(solution)/shard_map/ppermute | solution.py:20
  70.7 7.9 %collective-permute-start.2 = (f32[5,386,1]{1,2,0:T(1,128)S(1)}, f32[5,386,1]{1,2,0:T(1,128)S(1)}, u32[]{:S(2)}, u32[]{:S(2)}) collective-permute-start(f32[5,386,1]{1,2,0:T(1,128)S(1)} %copy.43), channel_id=1, source_target_pairs={{0,1},{1,2},{2,3},{4,5},{5,6},{6,7},{8,9},{9,10},{10,11},{12,13},{... | collective-permute-start | bytes 23168 | tf_op jit(solution)/shard_map/ppermute | solution.py:18
  206.6 15.5 %copy-start.2 = (f32[1,128,3,128,3]{3,1,4,2,0:T(8,128)S(1)}, f32[1,128,3,128,3]{3,1,4,2,0:T(8,128)}, u32[]{:S(2)}) copy-start(f32[1,128,3,128,3]{3,1,4,2,0:T(8,128)} %copy.49) | copy-start | bytes 1769476
  223.5 26.6 %copy-start.1 = (s32[2,2]{1,0:T(2,128)S(1)}, s32[2,2]{1,0:T(2,128)}, u32[]{:S(2)}) copy-start(s32[2,2]{1,0:T(2,128)} %param.7) | copy-start | bytes 52
  226.8 22.6 %copy-start.3 = (f32[3,128,128]{2,1,0:T(8,128)S(1)}, f32[3,128,128]{2,1,0:T(8,128)}, u32[]{:S(2)}) copy-start(f32[3,128,128]{2,1,0:T(8,128)} %param.11) | copy-start | bytes 589828
  226.8 13.3 %collective-permute-start.4 = (f32[4,256,128]{2,1,0:T(8,128)S(1)}, f32[4,256,128]{2,1,0:T(8,128)S(1)}, u32[]{:S(2)}, u32[]{:S(2)}) collective-permute-start(f32[4,256,128]{2,1,0:T(8,128)S(1)} %slice.343), channel_id=1, source_target_pairs={{0,1},{1,2},{2,3},{4,5},{5,6},{6,7},{8,9},{9,10},{10,11},{12,13},{... | collective-permute-start | bytes 1572872 | tf_op jit(solution)/shard_map/ppermute | solution.py:30
  240.2 9.2 %collective-permute-start.5 = (f32[4,128,128]{2,1,0:T(8,128)S(1)}, f32[4,128,128]{2,1,0:T(8,128)S(1)}, u32[]{:S(2)}, u32[]{:S(2)}) collective-permute-start(f32[4,128,128]{2,1,0:T(8,128)S(1)} %slice.345), channel_id=1, source_target_pairs={{0,4},{4,8},{8,12},{12,16},{16,20},{20,24},{24,28},{1,5},{5,9},{9,... | collective-permute-start | bytes 786440 | tf_op jit(solution)/shard_map/ppermute | solution.py:30
where the time goes:
time: 251 us; the launch traced here: 250 us
  local copies, waits for them, and re-layouts  138 us (55%)
  waiting for transfers between devices  56.3 us (22%)
  other arithmetic  25.5 us (10%)
  starting transfers between devices  25.1 us (10%)
  between operations  4.88 us (2%)
    another operation x6, local copies, waits for them, and re-layouts, advance(): return jnp.stack(results)  121 us
    all_to_all x1, waiting for transfers between devices, local(): lax.all_to_all(flattened, ('row', 'col'), split_axis=1, concat_axis=1, ti...  36.6 us
    ppermute x2, waiting for transfers between devices, passed_along(): return lax.ppermute(block, axis, route)  16 us
    ppermute x2, starting transfers between devices, padded_2(): lax.ppermute(head, axis, [((i + 1) % count, i) for i in range(ends)])  7.81 us
    all_to_all x1, starting transfers between devices, local(): lax.all_to_all(flattened, ('row', 'col'), split_axis=1, concat_axis=1, ti...  7.3 us
    concatenate x1, other arithmetic, padded_2(): jnp.concatenate([lax.ppermute(tail, axis, [(i, (i + 1) % count) for i in...  5.51 us
    ppermute x2, starting transfers between devices, passed_along(): return lax.ppermute(block, axis, route)  5.1 us
  transfers between devices with their start and end apart: 7, of which 4 were waited for; matrix products, arithmetic and copies ran while one was open for 3% of the time, Pallas kernels for 0%

commit v1 on v0

--- a/solution.py
+++ b/solution.py
@@ -106,7 +106,15 @@
         .transpose(0, 1, 3, 2, 4)
     )
     flattened = layered.reshape(3, tile_blocks * columns, band_rows, tile_cols)
-    arrived = lax.all_to_all(flattened, ("row", "col"), split_axis=1, concat_axis=1, tiled=True)
+    arrived = jnp.concatenate(
+        lax.all_to_all(
+            jnp.stack(jnp.split(flattened, lax.axis_size(("row", "col")), axis=1)),
+            ("row", "col"),
+            0,
+            0,
+        ),
+        axis=1,
+    )
     fields = arrived.reshape(3, tile_blocks * columns * band_rows, tile_cols)
     classes = bathy_index[0]
     wet_cells = wet_mask[0]

time: 251 us -> 260 us (1.036)
  local copies, waits for them, and re-layouts: 138 us -> 148 us
    unnamed x14 -> x29, local copies, waits for them, and re-layouts: 0.04 us -> 9.97 us
where the time goes in v1:
time: 260 us; the launch traced here: 259 us
  local copies, waits for them, and re-layouts  148 us (57%)
  waiting for transfers between devices  56.1 us (22%)
  other arithmetic  25.5 us (10%)
  starting transfers between devices  25 us (10%)
  between operations  4.89 us (2%)
    another operation x6, local copies, waits for them, and re-layouts, advance(): return jnp.stack(results)  121 us
    all_to_all x1, waiting for transfers between devices, local(): lax.all_to_all(jnp.stack(jnp.split(flattened, lax.axis_size(('row', 'col'...  36.5 us
    ppermute x2, waiting for transfers between devices, passed_along(): return lax.ppermute(block, axis, route)  16 us
    unnamed x29, local copies, waits for them, and re-layouts  9.97 us
    ppermute x2, starting transfers between devices, padded_2(): lax.ppermute(head, axis, [((i + 1) % count, i) for i in range(ends)])  7.81 us
    all_to_all x1, starting transfers between devices, local(): lax.all_to_all(jnp.stack(jnp.split(flattened, lax.axis_size(('row', 'col'...  7.3 us
    concatenate x1, other arithmetic, padded_2(): jnp.concatenate([lax.ppermute(tail, axis, [(i, (i + 1) % count) for i in...  5.51 us
  transfers between devices with their start and end apart: 7, of which 4 were waited for; matrix products, arithmetic and copies ran while one was open for 3% of the time, Pallas kernels for 0%

profile of v1, /device:TPU:12, one launch (start us, length us, event | category | flops | bytes accessed | tf_op | source)
XLA Modules:
  0.0 259.2 jit_solution(13016756139505442314)
XLA Ops:
  0.6 1.9 reshape_squeeze.3
  13.1 7.3 %all-to-all-start = ((f32[16,3,1,24,384]{4,3,1,2,0:T(8,128)}), f32[16,3,1,24,384]{4,3,1,2,0:T(8,128)}, u32[]{:S(2)}, u32[]{:S(2)}) async-start(f32[16,3,1,24,384]{4,3,1,2,0:T(8,128)} %fusion.43), calls=%async_computation | async-start | bytes 3538944 | tf_op jit(solution)/shard_map/all_to_all | solution.py:110
  22.7 36.5 %all-to-all-done = f32[16,3,1,24,384]{4,3,1,2,0:T(8,128)} async-done(((f32[16,3,1,24,384]{4,3,1,2,0:T(8,128)}), f32[16,3,1,24,384]{4,3,1,2,0:T(8,128)}, u32[]{:S(2)}, u32[]{:S(2)}) %all-to-all-start) | async-done | bytes 1769504 | tf_op jit(solution)/shard_map/all_to_all | solution.py:110
  59.2 1.6 copy.68
  60.8 3.1 %collective-permute-start.1 = (f32[5,1,384]{2,1,0:T(1,128)S(1)}, f32[5,1,384]{2,1,0:T(1,128)S(1)}, u32[]{:S(2)}, u32[]{:S(2)}) collective-permute-start(f32[5,1,384]{2,1,0:T(1,128)S(1)} %get-tuple-element.23), channel_id=1, source_target_pairs={{4,0},{8,4},{12,8},{5,1},{9,5},{13,9},{6,2},{10,6},{14,10},{7,3},{... | collective-permute-start | bytes 23048 | tf_op jit(solution)/shard_map/ppermute | solution.py:20
  63.9 2.8 %collective-permute-start = (f32[5,1,384]{2,1,0:T(1,128)S(1)}, f32[5,1,384]{2,1,0:T(1,128)S(1)}, u32[]{:S(2)}, u32[]{:S(2)}) collective-permute-start(f32[5,1,384]{2,1,0:T(1,128)S(1)} %get-tuple-element.22), channel_id=1, source_target_pairs={{0,4},{4,8},{8,12},{1,5},{5,9},{9,13},{2,6},{6,10},{10,14},{3,7},{... | collective-permute-start | bytes 23048 | tf_op jit(solution)/shard_map/ppermute | solution.py:18
  66.7 3.6 %collective-permute-done = f32[5,1,384]{2,1,0:T(1,128)S(1)} collective-permute-done((f32[5,1,384]{2,1,0:T(1,128)S(1)}, f32[5,1,384]{2,1,0:T(1,128)S(1)}, u32[]{:S(2)}, u32[]{:S(2)}) %collective-permute-start) | collective-permute-done | bytes 7712 | tf_op jit(solution)/shard_map/ppermute | solution.py:18
  70.3 1.6 pad_maximum_fusion.5
  71.9 1.6 copy.74
  73.5 4.7 %collective-permute-start.3 = (f32[5,386,1]{1,2,0:T(1,128)S(1)}, f32[5,386,1]{1,2,0:T(1,128)S(1)}, u32[]{:S(2)}, u32[]{:S(2)}) collective-permute-start(f32[5,386,1]{1,2,0:T(1,128)S(1)} %copy.74), channel_id=1, source_target_pairs={{1,0},{2,1},{3,2},{5,4},{6,5},{7,6},{9,8},{10,9},{11,10},{13,12},{... | collective-permute-start | bytes 23168 | tf_op jit(solution)/shard_map/ppermute | solution.py:20
  78.3 1.6 copy.73
  79.9 2.1 collective-permute-start.2
  86.5 1.3 copy.76
  87.8 1.4 copy.75
  89.2 5.5 %pad_maximum_fusion = f32[5,386,386]{2,1,0:T(8,128)S(1)} fusion(f32[5,386,1]{2,1,0:T(8,128)} %copy.76, f32[5,1,384]{2,1,0:T(1,128)S(1)} %collective-permute-done.1, f32[1,384,384]{2,1,0:T(8,128)S(1)} %copy.72, f32[1,384,384]{2,1,0:T(8,128)S(1)} %copy.71, f32[3,384,384]{2,1,0:T(8,128)S(1)} %bitcast.130, f32[5,1,384]{2,1,0:T(1,128)S(1)} %collective-permute-done, ...), kind=kLoop, calls=%fused_computation | loop fusion | flops 4469880 | bytes 5959840 | tf_op jit(solution)/shard_map/concatenate | solution.py:16
  96.0 2.2 fusion.22
  98.2 1.9 fusion.10
  100.1 2.8 %fusion.18 = (f32[385,384]{1,0:T(8,128)}, f32[385,384]{1,0:T(8,128)S(1)}, f32[385,384]{1,0:T(8,128)S(1)}) fusion(f32[385,384]{1,0:T(8,128)S(1)} %get-tuple-element.7, f32[386,386]{1,0:T(8,128)S(1)} %get-tuple-element.15, f32[386,386]{1,0:T(8,128)S(1)} %get-tuple-element.10, f32[386,386]{1,0:T(8,128)S(1)} %get-tuple-element.14, ...), kind=kLoop, calls=%fused_computation.49 | loop fusion | flops 2365440 | bytes 9461760 | tf_op jit(solution)/shard_map/mul | solution.py:67
  102.9 2.7 %fusion.7 = (f32[384,385]{1,0:T(8,128)}, f32[384,385]{1,0:T(8,128)S(1)}, f32[384,385]{1,0:T(8,128)}) fusion(f32[384,385]{1,0:T(8,128)S(1)} %get-tuple-element.5, f32[386,386]{1,0:T(8,128)S(1)} %get-tuple-element.8, f32[386,386]{1,0:T(8,128)S(1)} %get-tuple-element.15, f32[386,386]{1,0:T(8,128)S(1)} %get-tuple-element.13, ...), kind=kLoop, calls=%fused_computation.32 | loop fusion | flops 2365440 | bytes 9461760 | tf_op jit(solution)/shard_map/mul | solution.py:63
  106.2 25.2 %stack.94 = f32[1,128,3,128,3]{4,3,2,1,0:T(8,128)} reshape(f32[384,384]{1,0:T(8,128)S(1)} %fusion.26) | data formatting | bytes 1179648 | tf_op jit(solution)/shard_map/stack | solution.py:79
  131.4 15.5 %copy.79 = f32[1,128,3,128,3]{3,1,4,2,0:T(8,128)} copy(f32[1,128,3,128,3]{4,3,2,1,0:T(8,128)} %stack.94) | data formatting | bytes 1179648 | tf_op jit(solution)/shard_map/stack | solution.py:79
  146.8 3.8 %fusion.39 = (f32[384,384]{1,0:T(8,128)S(1)}, f32[384,384]{1,0:T(8,128)S(1)}) fusion(f32[385,384]{1,0:T(8,128)} %get-tuple-element.6, f32[384,385]{1,0:T(8,128)} %get-tuple-element.4, f32[386,386]{1,0:T(8,128)S(1)} %get-tuple-element.19, f32[384,385]{1,0:T(8,128)} %get-tuple-element.30, f32[385,384]{1,0:T(8,128)} %get-tuple-element.26, ...), kind=kLoop, calls=%fused_computation.81 | loop fusion | flops 2506752 | bytes 8257536 | tf_op jit(solution)/shard_map/sub | solution.py:72
  150.7 25.2 %stack.93 = f32[1,128,3,128,3]{4,3,2,1,0:T(8,128)} reshape(f32[384,384]{1,0:T(8,128)S(1)} %get-tuple-element.29) | data formatting | bytes 1179648 | tf_op jit(solution)/shard_map/stack | solution.py:79
  175.9 14.8 %copy.78 = f32[1,128,3,128,3]{3,1,4,2,0:T(8,128)S(1)} copy(f32[1,128,3,128,3]{4,3,2,1,0:T(8,128)} %stack.93) | data formatting | bytes 1179648 | tf_op jit(solution)/shard_map/stack | solution.py:79
  190.6 25.2 %stack.92 = f32[1,128,3,128,3]{4,3,2,1,0:T(8,128)} reshape(f32[384,384]{1,0:T(8,128)S(1)} %get-tuple-element.28) | data formatting | bytes 1179648 | tf_op jit(solution)/shard_map/stack | solution.py:79
  215.8 15.5 %copy.77 = f32[1,128,3,128,3]{3,1,4,2,0:T(8,128)} copy(f32[1,128,3,128,3]{4,3,2,1,0:T(8,128)} %stack.92) | data formatting | bytes 1179648 | tf_op jit(solution)/shard_map/stack | solution.py:79
  232.7 3.3 %dynamic_update_slice.3 = f32[4,256,256]{2,1,0:T(8,128)S(1)} dynamic-update-slice(f32[4,256,256]{2,1,0:T(8,128)S(1)} %broadcast_in_dim.46, f32[4,128,128]{2,1,0:T(8,128)S(1)} %concatenate.16, s32[]{:T(128)} %constant.5.clone.1, s32[]{:T(128)S(6)} %select_n.21, s32[]{:T(128)S(6)} %select_n.22) | dynamic-update-slice | bytes 524292 | tf_op jit(solution)/shard_map/dynamic_update_slice | solution.py:137
  236.0 2.5 collective-permute-start.4
  238.5 10.6 %collective-permute-done.4 = f32[4,256,128]{2,1,0:T(8,128)S(1)} collective-permute-done((f32[4,256,128]{2,1,0:T(8,128)S(1)}, f32[4,256,128]{2,1,0:T(8,128)S(1)}, u32[]{:S(2)}, u32[]{:S(2)}) %collective-permute-start.4) | collective-permute-done | bytes 524320 | tf_op jit(solution)/shard_map/ppermute | solution.py:30
  249.3 2.5 collective-permute-start.5
  251.8 1.3 maximum_bitcast_fusion
  253.1 5.3 %collective-permute-done.5 = f32[4,128,128]{2,1,0:T(8,128)S(1)} collective-permute-done((f32[4,128,128]{2,1,0:T(8,128)S(1)}, f32[4,128,128]{2,1,0:T(8,128)S(1)}, u32[]{:S(2)}, u32[]{:S(2)}) %collective-permute-start.5) | collective-permute-done | bytes 262176 | tf_op jit(solution)/shard_map/ppermute | solution.py:30
  (65 shorter events, 17.5 us)
Async XLA Ops:
  0.6 66.0 %copy-start = (s32[2,2]{1,0:T(2,128)S(1)}, s32[2,2]{1,0:T(2,128)}, u32[]{:S(2)}) copy-start(s32[2,2]{1,0:T(2,128)} %param.7) | copy-start | bytes 52
  13.1 7.3 %copy-start.4 = (s32[1,128,128]{2,1,0:T(8,128)S(1)}, s32[1,128,128]{2,1,0:T(8,128)}, u32[]{:S(2)}) copy-start(s32[1,128,128]{2,1,0:T(8,128)} %param.8) | copy-start | bytes 196612
  13.1 46.1 %all-to-all-start = ((f32[16,3,1,24,384]{4,3,1,2,0:T(8,128)}), f32[16,3,1,24,384]{4,3,1,2,0:T(8,128)}, u32[]{:S(2)}, u32[]{:S(2)}) async-start(f32[16,3,1,24,384]{4,3,1,2,0:T(8,128)} %fusion.43), calls=%async_computation | async-start | bytes 3538944 | tf_op jit(solution)/shard_map/all_to_all | solution.py:110
  20.7 0.8 copy-start.5
  20.7 0.8 copy-start.6
  60.8 5.9 %collective-permute-start.1 = (f32[5,1,384]{2,1,0:T(1,128)S(1)}, f32[5,1,384]{2,1,0:T(1,128)S(1)}, u32[]{:S(2)}, u32[]{:S(2)}) collective-permute-start(f32[5,1,384]{2,1,0:T(1,128)S(1)} %get-tuple-element.23), channel_id=1, source_target_pairs={{4,0},{8,4},{12,8},{5,1},{9,5},{13,9},{6,2},{10,6},{14,10},{7,3},{... | collective-permute-start | bytes 23048 | tf_op jit(solution)/shard_map/ppermute | solution.py:20
  63.9 6.4 %collective-permute-start = (f32[5,1,384]{2,1,0:T(1,128)S(1)}, f32[5,1,384]{2,1,0:T(1,128)S(1)}, u32[]{:S(2)}, u32[]{:S(2)}) collective-permute-start(f32[5,1,384]{2,1,0:T(1,128)S(1)} %get-tuple-element.22), channel_id=1, source_target_pairs={{0,4},{4,8},{8,12},{1,5},{5,9},{9,13},{2,6},{6,10},{10,14},{3,7},{... | collective-permute-start | bytes 23048 | tf_op jit(solution)/shard_map/ppermute | solution.py:18
  73.5 12.9 %collective-permute-start.3 = (f32[5,386,1]{1,2,0:T(1,128)S(1)}, f32[5,386,1]{1,2,0:T(1,128)S(1)}, u32[]{:S(2)}, u32[]{:S(2)}) collective-permute-start(f32[5,386,1]{1,2,0:T(1,128)S(1)} %copy.74), channel_id=1, source_target_pairs={{1,0},{2,1},{3,2},{5,4},{6,5},{7,6},{9,8},{10,9},{11,10},{13,12},{... | collective-permute-start | bytes 23168 | tf_op jit(solution)/shard_map/ppermute | solution.py:20
  79.9 7.9 %collective-permute-start.2 = (f32[5,386,1]{1,2,0:T(1,128)S(1)}, f32[5,386,1]{1,2,0:T(1,128)S(1)}, u32[]{:S(2)}, u32[]{:S(2)}) collective-permute-start(f32[5,386,1]{1,2,0:T(1,128)S(1)} %copy.73), channel_id=1, source_target_pairs={{0,1},{1,2},{2,3},{4,5},{5,6},{6,7},{8,9},{9,10},{10,11},{12,13},{... | collective-permute-start | bytes 23168 | tf_op jit(solution)/shard_map/ppermute | solution.py:18
  215.8 15.5 %copy-start.2 = (f32[1,128,3,128,3]{3,1,4,2,0:T(8,128)S(1)}, f32[1,128,3,128,3]{3,1,4,2,0:T(8,128)}, u32[]{:S(2)}) copy-start(f32[1,128,3,128,3]{3,1,4,2,0:T(8,128)} %copy.79) | copy-start | bytes 1769476
  236.0 13.1 %collective-permute-start.4 = (f32[4,256,128]{2,1,0:T(8,128)S(1)}, f32[4,256,128]{2,1,0:T(8,128)S(1)}, u32[]{:S(2)}, u32[]{:S(2)}) collective-permute-start(f32[4,256,128]{2,1,0:T(8,128)S(1)} %slice.343), channel_id=1, source_target_pairs={{0,1},{1,2},{2,3},{4,5},{5,6},{6,7},{8,9},{9,10},{10,11},{12,13},{... | collective-permute-start | bytes 1572872 | tf_op jit(solution)/shard_map/ppermute | solution.py:30
  249.3 9.2 %collective-permute-start.5 = (f32[4,128,128]{2,1,0:T(8,128)S(1)}, f32[4,128,128]{2,1,0:T(8,128)S(1)}, u32[]{:S(2)}, u32[]{:S(2)}) collective-permute-start(f32[4,128,128]{2,1,0:T(8,128)S(1)} %slice.345), channel_id=1, source_target_pairs={{0,4},{4,8},{8,12},{12,16},{16,20},{20,24},{24,28},{1,5},{5,9},{9,... | collective-permute-start | bytes 786440 | tf_op jit(solution)/shard_map/ppermute | solution.py:30
  251.7 7.5 %copy-start.1 = (s32[2,2]{1,0:T(2,128)S(1)}, s32[2,2]{1,0:T(2,128)}, u32[]{:S(2)}) copy-start(s32[2,2]{1,0:T(2,128)} %param.7) | copy-start | bytes 52
  251.7 6.7 %copy-start.3 = (f32[3,128,128]{2,1,0:T(8,128)S(1)}, f32[3,128,128]{2,1,0:T(8,128)}, u32[]{:S(2)}) copy-start(f32[3,128,128]{2,1,0:T(8,128)} %param.11) | copy-start | bytes 589828
